TPU v7x, 32 devices: a whole 2x2x4 slice. The times are simulated.
32 devices in a mesh: shard: 8 (over z, y), model: 4 (over x, core).
Axes of the slice: x: 2, y: 2, z: 4, core: 2. Of those that a mesh axis runs over, the one named last changes fastest.
Arguments:
- gradients: float32 [32, 128, 4096], P(None, 'shard', 'model'), may hold values from -6 to 6
- momentum: float32 [32, 128, 4096], P(None, 'shard', 'model'), may hold values from -6 to 6
- weights: float32 [32, 128, 4096], P(None, 'shard', 'model'), may hold values from -0.1875 to 0.1875
Outputs:
- new_weights: float32 [32, 128, 4096], P(None, 'shard', 'model')
- new_momentum: float32 [32, 128, 4096], P(None, 'shard', 'model')
All inputs are finite; a program needn't handle non-finite values.
Results may differ from a plain program's by a relative error of at most 0.00015.
Values sent between devices are 32-bit elements; how exact they have to be, the bound alone decides.
No kernel may reach another device: no remote copies, remote signals or barrier semaphores. Data moves between devices by JAX's collectives and lax.ppermute only.
A program may use at most 128 MiB of HBM per device.

v0:
```python
import jax
import jax.numpy as jnp
from jax import lax
from jax.sharding import PartitionSpec as P

ITERS = 4


hold_rate = 0.8
learn_rate = 1.0


def on_device(gradients, momentum, weights):
    new_momentum = hold_rate * momentum + gradients
    moved = lax.all_to_all(new_momentum, "shard", split_axis=0, concat_axis=1, tiled=True)
    whole = lax.all_to_all(moved, "model", split_axis=0, concat_axis=2, tiled=True)
    iterate = whole * lax.rsqrt(jnp.sum(whole * whole, axis=(1, 2), keepdims=True) + 1e-06)
    for step in range(ITERS):
        gram = jnp.einsum("mik,mjk->mij", iterate, iterate, precision=lax.Precision.HIGHEST)
        mixed = -4.775 * gram + 2.0315 * jnp.einsum(
            "mij,mjk->mik", gram, gram, precision=lax.Precision.HIGHEST
        )
        iterate = 3.4445 * iterate + jnp.einsum(
            "mij,mjk->mik", mixed, iterate, precision=lax.Precision.HIGHEST
        )
    iterate = lax.all_to_all(iterate, "model", split_axis=2, concat_axis=0, tiled=True)
    back = lax.all_to_all(iterate, "shard", split_axis=1, concat_axis=0, tiled=True)
    new_weights = weights - learn_rate * back
    return (new_weights, new_momentum)


def solution(mesh):
    placed = (P(None, "shard", "model"), P(None, "shard", "model"), P(None, "shard", "model"))
    return jax.shard_map(
        on_device,
        mesh=mesh,
        in_specs=placed,
        out_specs=(P(None, "shard", "model"), P(None, "shard", "model")),
        check_vma=False,
    )
```

profile of v0, /device:TPU:0, one launch (start us, length us, event | category | flops | bytes accessed | tf_op | source)
XLA Modules:
  0.0 208.4 jit_solution(6684310043670269516)
XLA Ops:
  0.6 2.7 %multiply_add_fusion = f32[32,16,1024]{2,1,0:T(8,128)S(1)} fusion(f32[32,16,1024]{2,1,0:T(8,128)} %param.3, f32[32,16,1024]{2,1,0:T(8,128)} %param.4), kind=kLoop, calls=%fused_computation.10 | loop fusion | flops 1048576 | bytes 6291456 | tf_op jit(solution)/shard_map/add | solution.py:14
  3.3 0.0 copy-start
  3.3 55.3 %all_to_all.63 = f32[32,16,1024]{2,1,0:T(8,128)S(1)} all-to-all(f32[32,16,1024]{2,1,0:T(8,128)S(1)} %multiply_add_fusion), channel_id=1, replica_groups=mesh['shard'=8,'model'=4] {'shard'}, dimensions={0} | all-to-all | bytes 4194304 | tf_op jit(solution)/shard_map/all_to_all | solution.py:15
  58.6 0.0 copy-done
  58.6 0.2 copy.30
  58.9 28.2 %all_to_all.64 = f32[4,128,1024]{2,1,0:T(8,128)S(1)} all-to-all(f32[4,128,1024]{2,1,0:T(8,128)S(1)} %bitcast.57), channel_id=1, replica_groups=mesh['shard'=8,'model'=4] {'model'}, dimensions={0} | all-to-all | bytes 4194304 | tf_op jit(solution)/shard_map/all_to_all | solution.py:16
  87.1 1.1 multiply_reduce_fusion
  88.9 1.8 fusion.4
  90.7 0.2 fusion.10
  91.0 2.6 %multiply_bitcast_fusion.1 = (f32[1,128,4,1024]{3,1,2,0:T(8,128)}, f32[1,128,4,1024]{3,1,2,0:T(8,128)}) fusion(f32[4,128,1024]{2,1,0:T(8,128)S(1)} %all_to_all.64, f32[]{:T(128)S(6)} %rsqrt.4), kind=kLoop, calls=%fused_computation.12 | loop fusion | flops 1048576 | bytes 6291460 | tf_op jit(solution)/shard_map/mul | solution.py:17
  93.5 1.9 copy.32
  95.4 2.9 %copy.31 = f32[1,128,4,1024]{1,3,2,0:T(8,128)} copy(f32[1,128,4,1024]{3,1,2,0:T(8,128)} %get-tuple-element.3) | data formatting | bytes 4194304 | tf_op jit(solution)/shard_map/mul | solution.py:23
  98.3 3.0 %copy.33 = f32[128,4096]{1,0:T(8,128)} copy(f32[128,4096]{0,1:T(8,128)} %bitcast.58) | data formatting | bytes 4194304 | tf_op jit(solution)/shard_map/mul | solution.py:23
  101.3 3.6 %convolution_add_fusion.3 = f32[128,4096]{1,0:T(8,128)S(1)} fusion(f32[128,4096]{1,0:T(8,128)} %copy.33, f32[128,128]{1,0:T(8,128)S(1)} %fusion.10, f32[128,4096]{0,1:T(8,128)S(1)} %bitcast.56), kind=kOutput, calls=%fused_computation.4 | convolution fusion | flops 805830656 | bytes 6356992 | tf_op jit(solution)/shard_map/mij,mjk->mik/dot_general | solution.py:23
  104.9 1.8 fusion.12
  106.7 0.2 fusion.9
  106.9 2.0 convolution_add_fusion.2
  108.9 1.8 fusion.13
  110.7 0.2 fusion.8
  110.9 2.0 convolution_add_fusion.1
  113.0 1.8 fusion.14
  114.8 0.2 fusion.7
  115.0 2.3 %fusion = f32[1,128,4096]{2,1,0:T(8,128)S(1)} fusion(f32[128,128]{1,0:T(8,128)S(1)} %fusion.7, f32[128,4096]{1,0:T(8,128)S(1)} %convolution_add_fusion.1), kind=kOutput, calls=%fused_computation.1 | convolution fusion | flops 806354944 | bytes 4259840 | tf_op jit(solution)/shard_map/mij,mjk->mik/dot_general | solution.py:23
  117.3 3.7 %copy.34 = f32[1,128,4096]{1,0,2:T(1,128)} copy(f32[1,128,4096]{2,1,0:T(8,128)S(1)} %fusion) | data formatting | bytes 4194304 | tf_op jit(solution)/shard_map/add | solution.py:23
  121.0 29.2 %all_to_all.65 = f32[1,128,4096]{1,0,2:T(1,128)S(1)} all-to-all(f32[1,128,4096]{1,0,2:T(1,128)} %copy.34), channel_id=1, replica_groups=mesh['shard'=8,'model'=4] {'model'}, dimensions={2} | all-to-all | bytes 4194304 | tf_op jit(solution)/shard_map/all_to_all | solution.py:26
  150.2 2.0 copy.35
  152.2 51.7 %all_to_all.66 = f32[4,128,1024]{2,0,1:T(4,128)S(1)} all-to-all(f32[4,128,1024]{2,0,1:T(4,128)} %copy.35), channel_id=1, replica_groups=mesh['shard'=8,'model'=4] {'shard'}, dimensions={1} | all-to-all | bytes 4194304 | tf_op jit(solution)/shard_map/all_to_all | solution.py:27
  203.8 1.2 copy.36
  205.1 0.0 copy-start.1
  205.1 0.2 copy.37
  205.3 1.3 copy-done.1
  206.6 1.7 bitcast_subtract_fusion
Async XLA Ops:
  3.3 55.4 %copy-start = (f32[32,16,1024]{2,1,0:T(8,128)}, f32[32,16,1024]{2,1,0:T(8,128)S(1)}, u32[]{:S(2)}) copy-start(f32[32,16,1024]{2,1,0:T(8,128)S(1)} %multiply_add_fusion) | copy-start | bytes 6291460
  205.1 1.6 copy-start.1
where the time goes:
time: 209 us; the launch traced here: 208 us
  blocking collectives  164 us (78%)
  matrix products  17.9 us (9%)
  local copies, waits for them, and re-layouts  16.4 us (8%)
  other arithmetic  8.09 us (4%)
    all_to_all x1, blocking collectives, on_device(): lax.all_to_all(new_momentum, 'shard', split_axis=0, concat_axis=1, tiled=...  55.3 us
    all_to_all x1, blocking collectives, on_device(): lax.all_to_all(iterate, 'shard', split_axis=1, concat_axis=0, tiled=True)  51.7 us
    all_to_all x1, blocking collectives, on_device(): lax.all_to_all(iterate, 'model', split_axis=2, concat_axis=0, tiled=True)  29.2 us
    all_to_all x1, blocking collectives, on_device(): lax.all_to_all(moved, 'model', split_axis=0, concat_axis=2, tiled=True)  28.2 us
    dot_general x4, matrix products, on_device(): jnp.einsum('mij,mjk->mik', mixed, iterate, precision=lax.Precision.HIGHEST)  9.94 us
    dot_general x4, matrix products, on_device(): jnp.einsum('mik,mjk->mij', iterate, iterate, precision=lax.Precision.HIGH...  7.17 us
    mul x2, local copies, waits for them, and re-layouts, on_device(): 3.4445 * iterate  5.84 us

commit v1 on v0

v1 whole, which is shorter than its diff:
```python
import jax
import jax.numpy as jnp
from jax import lax
from jax.sharding import PartitionSpec as P

ITERS = 4

hold_rate = 0.8
learn_rate = 1.0
HIGH = lax.Precision.HIGHEST


def mul(a, b):
    return jnp.einsum("mij,mjk->mik", a, b, precision=HIGH)


def direction(gram):
    eye = jnp.eye(gram.shape[-1], dtype=gram.dtype)
    squares = jnp.sum(gram * eye, axis=(1, 2), keepdims=True)
    scale = lax.rsqrt(squares + 1e-06)
    a = gram * scale * scale
    total = None
    for step in range(ITERS):
        q = 3.4445 * eye - 4.775 * a + 2.0315 * mul(a, a)
        total = q if total is None else mul(q, total)
        if step < ITERS - 1:
            a = mul(mul(q, a), q)
    return total * scale


def make(mesh):
    models = mesh.shape["model"]

    def on_device(gradients, momentum, weights):
        new_momentum = hold_rate * momentum + gradients
        whole = lax.all_to_all(new_momentum, "shard", split_axis=0, concat_axis=1, tiled=True)
        gram = jnp.einsum("mik,mjk->mij", whole, whole, precision=HIGH)
        mine = gram.shape[0] // models
        parts = lax.all_to_all(gram, "model", split_axis=0, concat_axis=0, tiled=True)
        gram = jnp.sum(parts.reshape(models, mine, *gram.shape[1:]), axis=0)
        turn = lax.all_gather(direction(gram), "model", axis=0, tiled=True)
        moved = mul(turn, whole)
        back = lax.all_to_all(moved, "shard", split_axis=1, concat_axis=0, tiled=True)
        new_weights = weights - learn_rate * back
        return (new_weights, new_momentum)

    return on_device


def solution(mesh):
    placed = P(None, "shard", "model")
    return jax.shard_map(
        make(mesh),
        mesh=mesh,
        in_specs=(placed, placed, placed),
        out_specs=(placed, placed),
        check_vma=False,
    )
```

time: 209 us -> 138 us (0.66)
  blocking collectives: 164 us -> 122 us
  local copies, waits for them, and re-layouts: 16.4 us -> 3.18 us
  matrix products: 17.9 us -> 6.62 us
  other arithmetic: 8.09 us -> 5.03 us
    all_to_all x3 -> x2, blocking collectives: 109 us -> 60.7 us  [the longest x1 52.1 us: on_device(): lax.all_to_all(moved, 'shard', split_axis=1, concat_axis=0, tiled=True)]
    dot_general x12 -> x15, matrix products: 17.9 us -> 6.62 us  [the longest x14 4.57 us: mul(): return jnp.einsum('mij,mjk->mik', a, b, precision=HIGH)]
    mul x3 -> x0, local copies, waits for them, and re-layouts: 7.74 us -> none  [the longest x2 5.84 us: on_device(): 3.4445 * iterate]
    all_gather x0 -> x1, blocking collectives: none -> 5.78 us  [on_device(): turn = lax.all_gather(direction(gram), 'model', axis=0, tiled=True)]
    add x1 -> x0, local copies, waits for them, and re-layouts: 3.7 us -> none  [on_device(): 3.4445 * iterate]
    mul x1 -> x0, other arithmetic: 2.56 us -> none  [on_device(): whole * lax.rsqrt(jnp.sum(whole * whole, axis=(1, 2), keepdims=True) + 1e...]
    all_to_all x3 -> x1, local copies, waits for them, and re-layouts: 3.41 us -> 1.2 us  [on_device(): lax.all_to_all(moved, 'shard', split_axis=1, concat_axis=0, tiled=True)]
where the time goes in v1:
time: 138 us
  blocking collectives  122 us (88%)
  matrix products  6.62 us (5%)
  other arithmetic  5.03 us (4%)
  local copies, waits for them, and re-layouts  3.18 us (2%)
  between operations  1.48 us (1%)
    all_to_all x1, blocking collectives, on_device(): lax.all_to_all(new_momentum, 'shard', split_axis=0, concat_axis=1, tiled=...  55.3 us
    all_to_all x1, blocking collectives, on_device(): lax.all_to_all(moved, 'shard', split_axis=1, concat_axis=0, tiled=True)  52.1 us
    all_to_all x1, blocking collectives, on_device(): lax.all_to_all(gram, 'model', split_axis=0, concat_axis=0, tiled=True)  8.57 us
    all_gather x1, blocking collectives, on_device(): turn = lax.all_gather(direction(gram), 'model', axis=0, tiled=True)  5.78 us
    dot_general x14, matrix products, mul(): return jnp.einsum('mij,mjk->mik', a, b, precision=HIGH)  4.57 us

profile of v1, /device:TPU:0, one launch (start us, length us, event | category | flops | bytes accessed | tf_op | source)
XLA Modules:
  0.0 138.1 jit_solution(6963360470699167812)
XLA Ops:
  0.6 2.7 %multiply_add_fusion = f32[32,16,1024]{2,1,0:T(8,128)S(1)} fusion(f32[32,16,1024]{2,1,0:T(8,128)} %param.3, f32[32,16,1024]{2,1,0:T(8,128)} %param.4), kind=kLoop, calls=%fused_computation.1 | loop fusion | flops 1048576 | bytes 6291456 | tf_op jit(solution)/shard_map/add | solution.py:35
  3.3 0.0 copy-start
  3.3 55.3 %all_to_all.41 = f32[32,16,1024]{2,1,0:T(8,128)S(1)} all-to-all(f32[32,16,1024]{2,1,0:T(8,128)S(1)} %multiply_add_fusion), channel_id=1, replica_groups=mesh['shard'=8,'model'=4] {'shard'}, dimensions={0} | all-to-all | bytes 4194304 | tf_op jit(solution)/shard_map/all_to_all | solution.py:36
  58.6 0.0 copy-done
  58.6 0.2 copy.7
  58.9 2.1 %fusion.7 = f32[4,128,128]{2,1,0:T(8,128)S(1)} fusion(f32[4,128,1024]{2,1,0:T(8,128)S(1)} %bitcast.37), kind=kOutput, calls=%fused_computation.21 | convolution fusion | flops 805306368 | bytes 2359296 | tf_op jit(solution)/shard_map/mik,mjk->mij/dot_general | solution.py:37
  60.9 8.6 %all_to_all.42 = f32[4,128,128]{2,1,0:T(8,128)S(1)} all-to-all(f32[4,128,128]{2,1,0:T(8,128)S(1)} %fusion.7), channel_id=1, replica_groups=mesh['shard'=8,'model'=4] {'model'}, dimensions={0} | all-to-all | bytes 524288 | tf_op jit(solution)/shard_map/all_to_all | solution.py:39
  69.5 0.6 select_reduce_fusion
  70.8 0.2 fusion.3
  71.1 0.2 fusion.4
  71.3 0.2 fusion.8
  71.5 0.2 fusion.2
  71.7 0.2 fusion.13
  71.9 0.2 fusion.9
  72.1 0.2 fusion.10
  72.3 0.2 fusion.1
  72.5 0.2 fusion.11
  72.8 0.2 fusion.14
  73.0 0.2 fusion.12
  73.2 0.2 fusion
  73.4 0.2 convolution_multiply_fusion
  73.6 5.8 %all-gather = f32[512,128]{1,0:T(8,128)S(1)} all-gather(f32[128,128]{1,0:T(8,128)S(1)} %convolution_multiply_fusion), channel_id=2, replica_groups=mesh['shard'=8,'model'=4] {'model'}, dimensions={0}, use_global_device_ids=true | all-gather | bytes 327680 | tf_op jit(solution)/shard_map/all_gather | solution.py:41
  79.4 1.9 %fusion.15 = f32[4,128,1024]{2,1,0:T(8,128)S(1)} fusion(f32[4,128,128]{2,1,0:T(8,128)S(1)} %bitcast.41, f32[4,128,1024]{2,1,0:T(8,128)S(1)} %bitcast.38), kind=kOutput, calls=%fused_computation.29 | convolution fusion | flops 805306368 | bytes 4456448 | tf_op jit(solution)/shard_map/mij,mjk->mik/dot_general | solution.py:14
  81.3 1.4 copy.8
  82.7 52.1 %all_to_all.43 = f32[4,128,1024]{2,0,1:T(4,128)S(1)} all-to-all(f32[4,128,1024]{2,0,1:T(4,128)S(1)} %copy.8), channel_id=1, replica_groups=mesh['shard'=8,'model'=4] {'shard'}, dimensions={1} | all-to-all | bytes 4194304 | tf_op jit(solution)/shard_map/all_to_all | solution.py:43
  134.8 0.0 copy-start.1
  134.8 1.2 copy.9
  136.0 0.4 copy-done.1
  136.3 1.7 %bitcast_subtract_fusion = f32[32,16,1024]{2,1,0:T(8,128)} fusion(f32[32,16,1024]{2,1,0:T(8,128)S(1)} %copy-done.1, f32[8,4,16,1024]{3,2,1,0:T(8,128)S(1)} %copy.9), kind=kLoop, calls=%fused_computation | loop fusion | flops 524288 | bytes 6291456 | tf_op jit(solution)/shard_map/sub | solution.py:44
  (1 shorter events, 0.0 us)
Async XLA Ops:
  3.3 55.4 %copy-start = (f32[32,16,1024]{2,1,0:T(8,128)}, f32[32,16,1024]{2,1,0:T(8,128)S(1)}, u32[]{:S(2)}) copy-start(f32[32,16,1024]{2,1,0:T(8,128)S(1)} %multiply_add_fusion) | copy-start | bytes 6291460
  134.8 1.6 %copy-start.1 = (f32[32,16,1024]{2,1,0:T(8,128)S(1)}, f32[32,16,1024]{2,1,0:T(8,128)}, u32[]{:S(2)}) copy-start(f32[32,16,1024]{2,1,0:T(8,128)} %param.5) | copy-start | bytes 6291460
